TPU v7x, 512 devices: a 4x2x32 block of a 4x8x32 slice. The times are simulated.
512 devices in a mesh: groups: 2 (over y), gx: 32 (over z), gy: 4 (over x), gz: 2 (over core).
Axes of the slice: x: 4, y: 2, z: 32, core: 2. Of those that a mesh axis runs over, the one named last changes fastest.
The devices are a block of a 4x8x32 slice.
Arguments:
- coords: float32 [64, 16, 16, 3, 128], P(('groups', 'gx'), 'gy', 'gz'), parts along dimension 0, may hold values from 0 to 1.1
- charges: float32 [64, 16, 16, 128], P(('groups', 'gx'), 'gy', 'gz'), parts along dimension 0, may hold values from -2 to 2
- atom_types: int32 [64, 16, 16, 128], P(('groups', 'gx'), 'gy', 'gz'), parts along dimension 0, may hold values from 0 to 63
- counts: int32 [64, 16, 16], P(('groups', 'gx'), 'gy', 'gz'), parts along dimension 0, may hold values from 64 to 128
- c6_table: float32 [64, 64], replicated, may hold values from 0.0001 to 0.001
- c12_table: float32 [64, 64], replicated, may hold values from 1e-08 to 1e-07
Outputs:
- forces: float32 [64, 16, 16, 3, 128], P(('groups', 'gx'), 'gy', 'gz'), parts along dimension 0
- energy: float32 [2], P('groups'), parts along dimension 0
There are 2 independent parts, one for each index of `groups`. A program takes and returns all parts, laid end to end along the dimension named above; an argument that names none is the same for every part. Nothing has to cross between parts.
All inputs are finite; a program needn't handle non-finite values.
Results may differ from a plain program's by a relative error of at most 0.0003.
Values sent between devices are 32-bit elements; how exact they have to be, the bound alone decides.
A program may use at most 64 MiB of HBM per device.

v0:
```python
import jax
import jax.numpy as jnp
from jax import lax
from jax.sharding import PartitionSpec as P

CELL_EDGE = 1.1
CUT_SQUARE = 1.0
SOFTEN = 0.09
ENERGY_UNIT = 0.1
CELL_PAIRS = (
    (0, 1),
    (0, 2),
    (0, 3),
    (0, 4),
    (0, 5),
    (0, 6),
    (0, 7),
    (1, 2),
    (1, 4),
    (2, 4),
    (1, 6),
    (2, 5),
    (4, 3),
)


def shifted(block, axis, distance):
    devices = range(lax.axis_size(axis))
    route = [((i - distance) % len(devices), i) for i in devices]
    return lax.ppermute(block, axis, route)


def over_axes(shard, axes):
    for axis in axes:
        shard = lax.psum(shard, axis)
    return shard


def corner_bits(corner_index):
    return (corner_index >> 2 & 1, corner_index >> 1 & 1, corner_index & 1)


def pack_cells(coords, charges, atom_types, counts):
    slot_count = coords.shape[-1]
    occupied = (jnp.arange(slot_count, dtype=jnp.int32) < counts[..., None]).astype(jnp.float32)
    return jnp.concatenate(
        [
            coords,
            charges[..., None, :],
            atom_types.astype(jnp.float32)[..., None, :],
            occupied[..., None, :],
        ],
        axis=3,
    )


def tile_terms(pack_a, pack_b, c6_sym, c12_sym, offset, pair_mask):
    type_ids = jnp.arange(c6_sym.shape[0]).astype(jnp.float32)
    type_hot_a = (pack_a[4][:, None] == type_ids[None, :]).astype(jnp.float32)
    type_hot_b = (pack_b[4][:, None] == type_ids[None, :]).astype(jnp.float32)
    c6_pair = jnp.dot(
        jnp.dot(type_hot_a, c6_sym, precision=lax.Precision.HIGHEST),
        type_hot_b.T,
        precision=lax.Precision.HIGHEST,
    )
    c12_pair = jnp.dot(
        jnp.dot(type_hot_a, c12_sym, precision=lax.Precision.HIGHEST),
        type_hot_b.T,
        precision=lax.Precision.HIGHEST,
    )
    charge_pair = pack_a[3][:, None] * pack_b[3][None, :]
    occupied_pair = pack_a[5][:, None] * pack_b[5][None, :] * pair_mask
    edge_inverse = 1.0 / (CUT_SQUARE + SOFTEN)
    edge_cube = edge_inverse**3

    def pair_energy(position_a, position_b):
        separation = position_b[:, None, :] - position_a[:, :, None] + offset[:, None, None]
        dist_square = jnp.sum(separation * separation, axis=0)
        inverse = 1.0 / (dist_square + SOFTEN)
        inverse_cube = inverse * inverse * inverse
        coulomb = charge_pair * (jnp.sqrt(inverse) - edge_inverse**0.5)
        dispersion = c12_pair * (inverse_cube * inverse_cube - edge_cube * edge_cube) - c6_pair * (
            inverse_cube - edge_cube
        )
        cutoff_taper = jnp.maximum(1.0 - dist_square / CUT_SQUARE, 0.0)
        return ENERGY_UNIT * jnp.sum(
            (coulomb + dispersion) * cutoff_taper * cutoff_taper * occupied_pair
        )

    energy, (grad_a, grad_b) = jax.value_and_grad(pair_energy, argnums=(0, 1))(
        pack_a[:3], pack_b[:3]
    )
    return (energy, -grad_a, -grad_b)


def cell_batch(packs_a, packs_b, c6_sym, c12_sym, offset, pair_mask):

    def single(tiles):
        return tile_terms(tiles[0], tiles[1], c6_sym, c12_sym, offset, pair_mask)

    return lax.map(single, (packs_a, packs_b), batch_size=8)


def on_device(coords, charges, atom_types, counts, c6_table, c12_table):
    c6_sym = 0.5 * (c6_table + c6_table.T)
    c12_sym = 0.5 * (c12_table + c12_table.T)
    packed = pack_cells(coords, charges, atom_types, counts)
    cells_x, cells_y, cells_z = packed.shape[:3]
    slot_count = packed.shape[-1]
    block_shape = (cells_x, cells_y, cells_z, 3, slot_count)
    upper_pairs = jnp.triu(jnp.ones((slot_count, slot_count), jnp.float32), 1)
    all_pairs = jnp.ones((slot_count, slot_count), jnp.float32)
    energy_sum = jnp.zeros((), jnp.float32)
    upper_rim = shifted(packed, "gx", -1)
    extended = jnp.concatenate([packed, upper_rim], axis=0)
    upper_rim = shifted(extended[:, :1], "gy", -1)
    extended = jnp.concatenate([extended, upper_rim], axis=1)
    upper_rim = shifted(extended[:, :, :1], "gz", -1)
    extended = jnp.concatenate([extended, upper_rim], axis=2)
    forces = jnp.zeros((cells_x + 1, cells_y + 1, cells_z + 1, 3, slot_count), jnp.float32)
    for source, target in ((0, 0),) + CELL_PAIRS:
        corner_a = corner_bits(source)
        corner_b = corner_bits(target)
        cells_a = extended[
            corner_a[0] : corner_a[0] + cells_x,
            corner_a[1] : corner_a[1] + cells_y,
            corner_a[2] : corner_a[2] + cells_z,
        ]
        cells_b = extended[
            corner_b[0] : corner_b[0] + cells_x,
            corner_b[1] : corner_b[1] + cells_y,
            corner_b[2] : corner_b[2] + cells_z,
        ]
        offset = jnp.array([(corner_b[k] - corner_a[k]) * CELL_EDGE for k in range(3)], jnp.float32)
        pair_mask = upper_pairs if source == target else all_pairs
        energies, force_a, force_b = cell_batch(
            cells_a.reshape((-1, 6, slot_count)),
            cells_b.reshape((-1, 6, slot_count)),
            c6_sym,
            c12_sym,
            offset,
            pair_mask,
        )
        forces = forces.at[
            corner_a[0] : corner_a[0] + cells_x,
            corner_a[1] : corner_a[1] + cells_y,
            corner_a[2] : corner_a[2] + cells_z,
        ].add(force_a.reshape(block_shape))
        forces = forces.at[
            corner_b[0] : corner_b[0] + cells_x,
            corner_b[1] : corner_b[1] + cells_y,
            corner_b[2] : corner_b[2] + cells_z,
        ].add(force_b.reshape(block_shape))
        energy_sum = energy_sum + jnp.sum(energies)
    returned = shifted(forces[:, :, cells_z:], "gz", 1)
    forces = forces[:, :, :cells_z].at[:, :, :1].add(returned)
    returned = shifted(forces[:, cells_y:], "gy", 1)
    forces = forces[:, :cells_y].at[:, :1].add(returned)
    returned = shifted(forces[cells_x:], "gx", 1)
    forces = forces[:cells_x].at[:1].add(returned)
    energy_sum = over_axes(energy_sum, ("gx", "gy", "gz"))
    return (forces, energy_sum.reshape(1))


def solution(mesh):
    return jax.shard_map(
        on_device,
        mesh=mesh,
        in_specs=(
            P(("groups", "gx"), "gy", "gz", None, None),
            P(("groups", "gx"), "gy", "gz", None),
            P(("groups", "gx"), "gy", "gz", None),
            P(("groups", "gx"), "gy", "gz"),
            P(),
            P(),
        ),
        out_specs=(P(("groups", "gx"), "gy", "gz", None, None), P("groups")),
        check_vma=False,
    )
```

profile of v0, /device:TPU:33, one launch (start us, length us, event | category | flops | bytes accessed | tf_op | source)
XLA Modules:
  0.0 442.4 jit_solution(17228414616098075159)
XLA Ops:
  3.0 45.9 %collective-permute-start = (f32[1,4,8,6,128]{4,2,3,1,0:T(8,128)S(1)}, f32[1,4,8,6,128]{4,2,3,1,0:T(8,128)S(1)}, u32[]{:S(2)}, u32[]{:S(2)}) collective-permute-start(f32[1,4,8,6,128]{4,2,3,1,0:T(8,128)S(1)} %pad_maximum_fusion.11), channel_id=1, source_target_pairs={{8,0},{16,8},{24,16},{32,24},{40,32},{48,40},{56,48},{64,56},{72,6... | collective-permute-start | bytes 294920 | tf_op jit(solution)/shard_map/ppermute | solution.py:30
  51.3 4.9 %collective-permute-start.1 = (f32[2,1,8,6,128]{4,2,3,1,0:T(8,128)S(1)}, f32[2,1,8,6,128]{4,2,3,1,0:T(8,128)S(1)}, u32[]{:S(2)}, u32[]{:S(2)}) collective-permute-start(f32[2,1,8,6,128]{4,2,3,1,0:T(8,128)S(1)} %pad_maximum_fusion.12), channel_id=1, source_target_pairs={{2,0},{4,2},{6,4},{0,6},{3,1},{5,3},{7,5},{1,7},{10,8},{12,10},{14... | collective-permute-start | bytes 147464 | tf_op jit(solution)/shard_map/ppermute | solution.py:30
  57.4 4.2 collective-permute-start.2
  61.7 18.7 %while.281 = (s32[]{:T(128)}, f32[4,8]{1,0:T(4,128)S(1)}, f32[4,8,3,128]{3,1,2,0:T(8,128)S(1)}, f32[4,8,3,128]{3,1,2,0:T(8,128)S(1)}, f32[4,8,6,128]{3,1,2,0:T(8...) while((s32[]{:T(128)}, f32[4,8]{1,0:T(4,128)S(1)}, ...), condition=%wide.region_65.66_spmd.clone, body=%wide.region_60.65_spmd.sunk.clone.sunk | while | flops 312996928 | bytes 4662845 | solution.py:101
  81.6 23.4 %while.285 = (s32[]{:T(128)}, f32[4,8]{1,0:T(4,128)}, f32[4,8,3,128]{3,1,2,0:T(8,128)S(1)}, f32[4,8,3,128]{3,1,2,0:T(8,128)S(1)}, f32[4,8,6,128]{3,1,2,0:T(8,128...) while((s32[]{:T(128)}, f32[4,8]{1,0:T(4,128)}, ...), condition=%wide.region_5.6_spmd.clone.clone, body=%wide.region_0.5_spmd.sunk.clone.clone.sunk | while | flops 312374336 | bytes 4638225 | solution.py:101
  105.6 18.9 %while.272 = (s32[]{:T(128)}, f32[4,8]{1,0:T(4,128)S(1)}, f32[4,8,3,128]{3,1,2,0:T(8,128)S(1)}, f32[4,8,3,128]{3,1,2,0:T(8,128)S(1)}, f32[4,8,6,128]{3,1,2,0:T(8...) while((s32[]{:T(128)}, f32[4,8]{1,0:T(4,128)S(1)}, ...), condition=%wide.region_11.12_spmd.clone, body=%wide.region_6.11_spmd.sunk.clone.sunk | while | flops 312996928 | bytes 4662845 | solution.py:101
  125.2 18.7 %while.273 = (s32[]{:T(128)}, f32[4,8]{1,0:T(4,128)S(1)}, f32[4,8,3,128]{3,1,2,0:T(8,128)S(1)}, f32[4,8,3,128]{3,1,2,0:T(8,128)S(1)}, f32[4,8,6,128]{3,1,2,0:T(8...) while((s32[]{:T(128)}, f32[4,8]{1,0:T(4,128)S(1)}, ...), condition=%wide.region_17.18_spmd.clone, body=%wide.region_12.17_spmd.sunk.clone.sunk | while | flops 312996928 | bytes 4662845 | solution.py:101
  144.5 18.9 %while.274 = (s32[]{:T(128)}, f32[4,8]{1,0:T(4,128)S(1)}, f32[4,8,3,128]{3,1,2,0:T(8,128)S(1)}, f32[4,8,3,128]{3,1,2,0:T(8,128)S(1)}, f32[4,8,6,128]{3,1,2,0:T(8...) while((s32[]{:T(128)}, f32[4,8]{1,0:T(4,128)S(1)}, ...), condition=%wide.region_23.24_spmd.clone, body=%wide.region_18.0_spmd.sunk.clone.sunk | while | flops 312996928 | bytes 4662845 | solution.py:101
  164.1 18.7 %while.275 = (s32[]{:T(128)}, f32[4,8]{1,0:T(4,128)S(1)}, f32[4,8,3,128]{3,1,2,0:T(8,128)S(1)}, f32[4,8,3,128]{3,1,2,0:T(8,128)S(1)}, f32[4,8,6,128]{3,1,2,0:T(8...) while((s32[]{:T(128)}, f32[4,8]{1,0:T(4,128)S(1)}, ...), condition=%wide.region_29.30_spmd.clone, body=%wide.region_24.29_spmd.sunk.clone.sunk | while | flops 312996928 | bytes 4662845 | solution.py:101
  183.4 19.2 %while.276 = (s32[]{:T(128)}, f32[4,8]{1,0:T(4,128)S(1)}, f32[4,8,3,128]{3,1,2,0:T(8,128)S(1)}, f32[4,8,3,128]{3,1,2,0:T(8,128)S(1)}, f32[4,8,6,128]{3,1,2,0:T(8...) while((s32[]{:T(128)}, f32[4,8]{1,0:T(4,128)S(1)}, ...), condition=%wide.region_35.36_spmd.clone, body=%wide.region_30.0_spmd.sunk.clone.sunk | while | flops 312996928 | bytes 4662845 | solution.py:101
  203.2 18.7 %while.277 = (s32[]{:T(128)}, f32[4,8]{1,0:T(4,128)S(1)}, f32[4,8,3,128]{3,1,2,0:T(8,128)S(1)}, f32[4,8,3,128]{3,1,2,0:T(8,128)S(1)}, f32[4,8,6,128]{3,1,2,0:T(8...) while((s32[]{:T(128)}, f32[4,8]{1,0:T(4,128)S(1)}, ...), condition=%wide.region_41.42_spmd.clone, body=%wide.region_36.41_spmd.sunk.clone.sunk | while | flops 312996928 | bytes 4662845 | solution.py:101
  221.9 18.8 %while.278 = (s32[]{:T(128)}, f32[4,8]{1,0:T(4,128)S(1)}, f32[4,8,3,128]{3,1,2,0:T(8,128)S(1)}, f32[4,8,3,128]{3,1,2,0:T(8,128)S(1)}, f32[4,8,6,128]{3,1,2,0:T(8...) while((s32[]{:T(128)}, f32[4,8]{1,0:T(4,128)S(1)}, ...), condition=%wide.region_47.48_spmd.clone, body=%wide.region_42.0_spmd.sunk.clone.sunk | while | flops 312996928 | bytes 4662813 | solution.py:101
  241.4 18.7 %while.279 = (s32[]{:T(128)}, f32[4,8]{1,0:T(4,128)S(1)}, f32[4,8,3,128]{3,1,2,0:T(8,128)S(1)}, f32[4,8,3,128]{3,1,2,0:T(8,128)S(1)}, f32[4,8,6,128]{3,1,2,0:T(8...) while((s32[]{:T(128)}, f32[4,8]{1,0:T(4,128)S(1)}, ...), condition=%wide.region_53.54_spmd.clone, body=%wide.region_48.53_spmd.sunk.clone.sunk | while | flops 312996928 | bytes 4662845 | solution.py:101
  260.3 18.9 %while.280 = (s32[]{:T(128)}, f32[4,8]{1,0:T(4,128)S(1)}, f32[4,8,3,128]{3,1,2,0:T(8,128)S(1)}, f32[4,8,3,128]{3,1,2,0:T(8,128)S(1)}, f32[4,8,6,128]{3,1,2,0:T(8...) while((s32[]{:T(128)}, f32[4,8]{1,0:T(4,128)S(1)}, ...), condition=%wide.region_59.60_spmd.clone, body=%wide.region_54.0_spmd.sunk.clone.sunk | while | flops 312996928 | bytes 4662845 | solution.py:101
  279.5 18.7 %while.282 = (s32[]{:T(128)}, f32[4,8]{1,0:T(4,128)S(1)}, f32[4,8,3,128]{3,1,2,0:T(8,128)S(1)}, f32[4,8,3,128]{3,1,2,0:T(8,128)S(1)}, f32[4,8,6,128]{3,1,2,0:T(8...) while((s32[]{:T(128)}, f32[4,8]{1,0:T(4,128)S(1)}, ...), condition=%wide.region_71.72_spmd.clone, body=%wide.region_66.71_spmd.sunk.clone.sunk | while | flops 312996928 | bytes 4662845 | solution.py:101
  298.8 18.9 %while.283 = (s32[]{:T(128)}, f32[4,8]{1,0:T(4,128)S(1)}, f32[4,8,3,128]{3,1,2,0:T(8,128)S(1)}, f32[4,8,3,128]{3,1,2,0:T(8,128)S(1)}, f32[4,8,6,128]{3,1,2,0:T(8...) while((s32[]{:T(128)}, f32[4,8]{1,0:T(4,128)S(1)}, ...), condition=%wide.region_77.78_spmd.clone, body=%wide.region_72.77_spmd.sunk.clone.sunk | while | flops 312996928 | bytes 4662845 | solution.py:101
  318.4 21.5 %while.284 = (s32[]{:T(128)}, f32[4,8]{1,0:T(4,128)S(1)}, f32[4,8,3,128]{3,1,2,0:T(8,128)S(1)}, f32[4,8,3,128]{3,1,2,0:T(8,128)S(1)}, f32[4,8,6,128]{3,1,2,0:T(8...) while((s32[]{:T(128)}, f32[4,8]{1,0:T(4,128)S(1)}, ...), condition=%wide.region_83.84_spmd.clone, body=%wide.region_78.83_spmd.sunk.clone.sunk | while | flops 312996928 | bytes 4662845 | solution.py:101
  340.2 2.0 collective-permute-start.3
  343.5 2.5 collective-permute-start.4
  346.0 3.9 collective-permute-done.4
  349.9 2.0 collective-permute-start.5
  370.2 43.0 %psum.21 = f32[]{:T(128)} all-reduce(f32[]{:T(128)S(6)} %add.945), channel_id=1, replica_groups=mesh['groups'=2,'gx'=32,'gy'=4,'gz'=2] {'gx'}, use_global_device_ids=true, to_apply=%region_98.99 | all-reduce | flops 1 | bytes 8 | tf_op jit(solution)/shard_map/psum | solution.py:35
  413.3 7.9 %psum.22 = f32[]{:T(128)} all-reduce(f32[]{:T(128)} %psum.21), channel_id=1, replica_groups=mesh['groups'=2,'gx'=32,'gy'=4,'gz'=2] {'gy'}, use_global_device_ids=true, to_apply=%region_99.100 | all-reduce | flops 1 | bytes 8 | tf_op jit(solution)/shard_map/psum | solution.py:35
  421.2 20.1 %psum.23 = f32[1]{0:T(128)} all-reduce(f32[1]{0:T(128)} %bitcast.41), channel_id=1, replica_groups=mesh['groups'=2,'gx'=32,'gy'=4,'gz'=2] {'gz'}, use_global_device_ids=true, to_apply=%region_100.101 | all-reduce | flops 1 | bytes 8 | tf_op jit(solution)/shard_map/psum | solution.py:35
  (1232 shorter events, 286.3 us)
Async XLA Ops:
  0.6 56.8 %copy-start.2 = (f32[1,4,8,128]{3,2,1,0:T(8,128)S(1)}, f32[1,4,8,128]{3,2,1,0:T(8,128)}, u32[]{:S(2)}) copy-start(f32[1,4,8,128]{3,2,1,0:T(8,128)} %param.113) | copy-start | bytes 49156
  0.6 56.8 %copy-start = (f32[1,4,8,3,128]{4,2,3,1,0:T(8,128)S(1)}, f32[1,4,8,3,128]{4,2,3,1,0:T(8,128)}, u32[]{:S(2)}) copy-start(f32[1,4,8,3,128]{4,2,3,1,0:T(8,128)} %param.112) | copy-start | bytes 147460
  0.7 55.6 %copy-start.7 = (f32[64,64]{1,0:T(8,128)S(1)}, f32[64,64]{1,0:T(8,128)}, u32[]{:S(2)}) copy-start(f32[64,64]{1,0:T(8,128)} %param.116) | copy-start | bytes 49156
  0.7 55.6 %copy-start.8 = (f32[64,64]{1,0:T(8,128)S(1)}, f32[64,64]{1,0:T(8,128)}, u32[]{:S(2)}) copy-start(f32[64,64]{1,0:T(8,128)} %param.117) | copy-start | bytes 49156
  3.0 47.5 %collective-permute-start = (f32[1,4,8,6,128]{4,2,3,1,0:T(8,128)S(1)}, f32[1,4,8,6,128]{4,2,3,1,0:T(8,128)S(1)}, u32[]{:S(2)}, u32[]{:S(2)}) collective-permute-start(f32[1,4,8,6,128]{4,2,3,1,0:T(8,128)S(1)} %pad_maximum_fusion.11), channel_id=1, source_target_pairs={{8,0},{16,8},{24,16},{32,24},{40,32},{48,40},{56,48},{64,56},{72,6... | collective-permute-start | bytes 294920 | tf_op jit(solution)/shard_map/ppermute | solution.py:30
  51.3 10.4 %copy-start.20 = (f32[3]{0:T(128)S(1)}, f32[3]{0:T(128)}, u32[]{:S(2)}) copy-start(f32[3]{0:T(128)} %constant.1683.clone..sunk.2) | copy-start | bytes 40
  51.3 6.1 %collective-permute-start.1 = (f32[2,1,8,6,128]{4,2,3,1,0:T(8,128)S(1)}, f32[2,1,8,6,128]{4,2,3,1,0:T(8,128)S(1)}, u32[]{:S(2)}, u32[]{:S(2)}) collective-permute-start(f32[2,1,8,6,128]{4,2,3,1,0:T(8,128)S(1)} %pad_maximum_fusion.12), channel_id=1, source_target_pairs={{2,0},{4,2},{6,4},{0,6},{3,1},{5,3},{7,5},{1,7},{10,8},{12,10},{14... | collective-permute-start | bytes 147464 | tf_op jit(solution)/shard_map/ppermute | solution.py:30
  57.4 23.0 %collective-permute-start.2 = (f32[2,5,1,6,128]{4,2,3,1,0:T(1,128)S(1)}, f32[2,5,1,6,128]{4,2,3,1,0:T(1,128)S(1)}, u32[]{:S(2)}, u32[]{:S(2)}) collective-permute-start(f32[2,5,1,6,128]{4,2,3,1,0:T(1,128)S(1)} %pad_maximum_fusion.16), channel_id=1, source_target_pairs={{1,0},{0,1},{3,2},{2,3},{5,4},{4,5},{7,6},{6,7},{9,8},{8,9},{11,10... | collective-permute-start | bytes 92168 | tf_op jit(solution)/shard_map/ppermute | solution.py:30
  80.4 1.2 copy-start.5
  80.4 1.2 copy-start.21
  125.2 18.7 %copy-start.17 = (f32[3]{0:T(128)S(1)}, f32[3]{0:T(128)}, u32[]{:S(2)}) copy-start(f32[3]{0:T(128)} %constant.1676.clone..sunk.2) | copy-start | bytes 40
  164.1 19.3 %copy-start.15 = (f32[3]{0:T(128)S(1)}, f32[3]{0:T(128)}, u32[]{:S(2)}) copy-start(f32[3]{0:T(128)} %constant.1678.clone..sunk.2) | copy-start | bytes 40
  241.4 18.9 %copy-start.12 = (f32[3]{0:T(128)S(1)}, f32[3]{0:T(128)}, u32[]{:S(2)}) copy-start(f32[3]{0:T(128)} %constant.1682.clone..sunk.2) | copy-start | bytes 40
  260.3 19.2 %copy-start.11 = (f32[3]{0:T(128)S(1)}, f32[3]{0:T(128)}, u32[]{:S(2)}) copy-start(f32[3]{0:T(128)} %constant.1684.clone..sunk.2) | copy-start | bytes 40
  279.4 18.8 %copy-start.4 = (f32[4,8,3,128]{3,1,2,0:T(8,128)S(1)}, f32[4,8,3,128]{3,1,2,0:T(8,128)}, u32[]{:S(2)}) copy-start(f32[4,8,3,128]{3,1,2,0:T(8,128)} %copy-done.3) | copy-start | bytes 147460
  279.4 18.8 %copy-start.6 = (f32[4,8,3,128]{3,1,2,0:T(8,128)S(1)}, f32[4,8,3,128]{3,1,2,0:T(8,128)}, u32[]{:S(2)}) copy-start(f32[4,8,3,128]{3,1,2,0:T(8,128)} %copy-done.5) | copy-start | bytes 147460
  340.0 11.9 %copy-start.22 = (f32[4,8]{1,0:T(4,128)S(1)}, f32[4,8]{1,0:T(4,128)}, u32[]{:S(2)}) copy-start(f32[4,8]{1,0:T(4,128)} %copy-done.21) | copy-start | bytes 388
  340.0 13.8 %copy-start.24 = (f32[4,8]{1,0:T(4,128)S(1)}, f32[4,8]{1,0:T(4,128)}, u32[]{:S(2)}) copy-start(f32[4,8]{1,0:T(4,128)} %copy-done.23) | copy-start | bytes 388
  340.0 15.7 %copy-start.26 = (f32[4,8]{1,0:T(4,128)S(1)}, f32[4,8]{1,0:T(4,128)}, u32[]{:S(2)}) copy-start(f32[4,8]{1,0:T(4,128)} %copy-done.25) | copy-start | bytes 388
  340.0 17.0 %copy-start.28 = (f32[4,8]{1,0:T(4,128)S(1)}, f32[4,8]{1,0:T(4,128)}, u32[]{:S(2)}) copy-start(f32[4,8]{1,0:T(4,128)} %copy-done.27) | copy-start | bytes 388
  340.0 18.2 %copy-start.30 = (f32[4,8]{1,0:T(4,128)S(1)}, f32[4,8]{1,0:T(4,128)}, u32[]{:S(2)}) copy-start(f32[4,8]{1,0:T(4,128)} %copy-done.29) | copy-start | bytes 388
  340.2 3.1 collective-permute-start.3
  343.5 6.4 %collective-permute-start.4 = (f32[2,1,8,3,128]{4,2,3,1,0:T(8,128)S(1)}, f32[2,1,8,3,128]{4,2,3,1,0:T(8,128)S(1)}, u32[]{:S(2)}, u32[]{:S(2)}) collective-permute-start(f32[2,1,8,3,128]{4,2,3,1,0:T(8,128)S(1)} %slice.2358), channel_id=1, source_target_pairs={{6,0},{0,2},{2,4},{4,6},{7,1},{1,3},{3,5},{5,7},{14,8},{8,10},{10,... | collective-permute-start | bytes 73736 | tf_op jit(solution)/shard_map/ppermute | solution.py:30
  349.9 91.4 %collective-permute-start.5 = (f32[1,4,8,3,128]{4,2,3,1,0:T(8,128)S(1)}, f32[1,4,8,3,128]{4,2,3,1,0:T(8,128)S(1)}, u32[]{:S(2)}, u32[]{:S(2)}) collective-permute-start(f32[1,4,8,3,128]{4,2,3,1,0:T(8,128)S(1)} %slice.2360), channel_id=1, source_target_pairs={{248,0},{0,8},{8,16},{16,24},{24,32},{32,40},{40,48},{48,56},{56,6... | collective-permute-start | bytes 147464 | tf_op jit(solution)/shard_map/ppermute | solution.py:30
  (13 other events, 8.4 us)
where the time goes:
time: 450 us; the launch traced here: 442 us
  matrix products  167 us (37%)
  other arithmetic  96.1 us (21%)
  blocking collectives  71.1 us (16%)
  starting transfers between devices  61.3 us (14%)
  local copies, waits for them, and re-layouts  20.9 us (5%)
  between operations  11.4 us (3%)
  loops' own time  8.36 us (2%)
  waiting for transfers between devices  6.18 us (1%)
    dot_general x56, matrix products, tile_terms(): jnp.dot(jnp.dot(type_hot_a, c12_sym, precision=lax.Precision.HIGHEST), ty...  92.9 us
    psum x3, blocking collectives, over_axes(): shard = lax.psum(shard, axis)  71.1 us
    ppermute x6, starting transfers between devices, shifted(): return lax.ppermute(block, axis, route)  61.3 us
    reduce_sum x56, other arithmetic, pair_energy(): position_b[:, None, :] - position_a[:, :, None] + offset[:, None, None]  55.2 us
    dot_general x56, matrix products, tile_terms(): jnp.dot(jnp.dot(type_hot_a, c6_sym, precision=lax.Precision.HIGHEST), typ...  35.5 us
    reduce_sum x56, other arithmetic, pair_energy(): dist_square = jnp.sum(separation * separation, axis=0)  26.7 us
    dot_general x56, matrix products, tile_terms(): jnp.dot(type_hot_a, c6_sym, precision=lax.Precision.HIGHEST)  19.3 us
    dot_general x56, matrix products, tile_terms(): jnp.dot(type_hot_a, c12_sym, precision=lax.Precision.HIGHEST)  19.3 us
  transfers between devices with their start and end apart: 6, of which 3 were waited for; matrix products, arithmetic and copies ran while one was open for 7% of the time, Pallas kernels for 0%

commit v1 on v0

v1 whole, which is shorter than its diff:
```python
import functools

import jax
import jax.numpy as jnp
import numpy as np
from jax import lax
from jax.experimental import pallas as pl
from jax.experimental.pallas import tpu as pltpu
from jax.sharding import PartitionSpec as P

CELL_EDGE = 1.1
SOFTEN = 0.09
ENERGY_UNIT = 0.1
EDGE_INVERSE = 1.0 / (1.0 + SOFTEN)
EDGE_ROOT = EDGE_INVERSE**0.5
EDGE_CUBE = EDGE_INVERSE**3
NEIGHBOURS = (
    (0, 0, 1),
    (0, 1, 0),
    (0, 1, 1),
    (1, 0, 0),
    (1, 0, 1),
    (1, 1, 0),
    (1, 1, 1),
    (0, 1, -1),
    (1, 0, -1),
    (1, 1, -1),
    (1, -1, 0),
    (1, -1, 1),
    (1, -1, -1),
)


def neighbour_lists(ny, nz):
    tiles, ranges = [], []
    empty = 2 * (ny + 1) * (nz + 1)
    for y in range(ny + 1):
        for z in range(nz + 1):
            p = y * (nz + 1) + z
            partners = [(p, 0)] if y < ny and z < nz else []
            for ox, oy, oz in NEIGHBOURS:
                low_y, low_z = y + min(oy, 0), z + min(oz, 0)
                if 0 <= low_y < ny and 0 <= low_z < nz:
                    partners.append(((ox * (ny + 1) + y + oy) * (nz + 1) + z + oz, -1024))
            if len(partners) % 2:
                partners.append((empty, -1024))
            ranges.append((len(tiles) // 2, len(partners) // 2))
            tiles += [(p, b, below) for b, below in partners]
    tiles.append((0, empty, 0))
    return np.array(tiles, np.int32).reshape(-1), np.array(ranges, np.int32).reshape(-1)


def split(value):
    high = value.astype(jnp.bfloat16)
    return high, (value - high.astype(jnp.float32)).astype(jnp.bfloat16)


def pair_kernel(
    shape, tile_ref, range_ref, raw_ref, table_ref, force_ref, energy_ref,
    pack_ref, col_ref, left_ref, right_ref, acc_a, acc_b, even_ref, odd_ref,
):
    iota = functools.partial(lax.broadcasted_iota, jnp.int32, (128, 128))
    row = lax.broadcasted_iota(jnp.int32, (8, 128), 0)
    cells_a, cells = shape[1] * shape[2], shape[0] * shape[1] * shape[2]

    for x in range(shape[0]):
        for y in range(shape[1]):
            for z in range(shape[2]):
                place = jnp.where(row == 0, x, jnp.where(row == 1, y, jnp.where(row == 2, z, 0)))
                pack_ref[(x * shape[1] + y) * shape[2] + z] = raw_ref[x, y, z] + CELL_EDGE * place
    pack_ref[cells] = jnp.where(row == 4, 64.0, 0.0)

    def prepare_a(p):
        turned = jnp.transpose(pack_ref[p])
        for f in range(3):
            col_ref[p, f] = jnp.broadcast_to(turned[:, f : f + 1], (128, 128))
        qa = jnp.broadcast_to(turned[:, 3:4], (128, 128))
        col_ref[p, 3] = qa * (1.0 / 6.0)
        kinds = jnp.broadcast_to(turned[:, 4:5], (128, 128))
        hot = jnp.where(kinds == iota(1).astype(jnp.float32), 1.0, 0.0).astype(jnp.bfloat16)
        rows = jnp.dot(
            jnp.concatenate([hot, hot], axis=1), table_ref[...], preferred_element_type=jnp.float32
        )
        r6, r12 = rows[:, :128], rows[:, 128:]
        low_half = iota(1) < 64
        empty = jnp.zeros((128, 128), jnp.bfloat16)

        def halves(value):
            high = value.astype(jnp.bfloat16).astype(jnp.float32)
            return jnp.where(low_half, high, value - high).astype(jnp.bfloat16)

        left_ref[p, :128, :128] = halves(r6)
        left_ref[p, :128, 128:] = empty
        left_ref[p, 128:256, :128] = halves(r12)
        left_ref[p, 128:256, 128:] = empty
        left_ref[p, 256:, :128] = halves(EDGE_CUBE * EDGE_CUBE * r12 - EDGE_CUBE * r6)
        qs = qa * EDGE_ROOT
        high = qs.astype(jnp.bfloat16).astype(jnp.float32)
        lane = iota(1)
        left_ref[p, 256:, 128:] = jnp.where(
            lane < 4, jnp.where((lane & 1) == 0, high, qs - high), 0.0
        ).astype(jnp.bfloat16)
        acc_a[p] = jnp.zeros((3, 128, 128), jnp.float32)

    def prepare_b(b):
        kinds = jnp.broadcast_to(pack_ref[b, pl.ds(4, 1), :].astype(jnp.int32), (128, 128))
        hot = jnp.where((iota(0) & 63) == kinds, 1.0, 0.0)
        right_ref[b, :128] = hot.astype(jnp.bfloat16)
        q = jnp.broadcast_to(pack_ref[b, pl.ds(3, 1), :], (16, 128))
        high = q.astype(jnp.bfloat16).astype(jnp.float32)
        row = lax.broadcasted_iota(jnp.int32, (16, 128), 0)
        q = jnp.where(row < 2, high, jnp.where(row < 4, q - high, 0.0))
        right_ref[b, 128:144] = q.astype(jnp.bfloat16)
        right_ref[b, 144:] = jnp.zeros((112, 128), jnp.bfloat16)
        acc_b[b] = jnp.zeros((3, 8, 128), jnp.float32)

    step = 3

    @pl.loop(0, cells_a // step)
    def _(i):
        for j in range(step):
            prepare_a(i * step + j)

    @pl.loop(0, cells // 5)
    def _(i):
        for j in range(5):
            prepare_b(i * 5 + j)

    prepare_b(cells)
    energy_ref[...] = jnp.zeros((8, 128), jnp.float32)

    def look_up(t, out_ref):
        p, b = tile_ref[3 * t], tile_ref[3 * t + 1]
        out_ref[...] = jnp.dot(left_ref[p], right_ref[b], preferred_element_type=jnp.float32)

    def tile(p, t, rows, in_ref, masked):
        b = tile_ref[3 * t + 1]
        xb, yb, zb, qb = (pack_ref[b, pl.ds(f, 1), :] for f in range(4))
        energy = jnp.zeros((8, 128), jnp.float32)
        other = [jnp.zeros((8, 128), jnp.float32)] * 3
        for first in range(0, rows, 8):
            at = slice(first, first + 8)
            xa, ya, za, qa = (col_ref[p, f, at, :] for f in range(4))
            c6 = in_ref[first : first + 8, :]
            c12 = in_ref[128 + first : 136 + first, :]
            edge = in_ref[256 + first : 264 + first, :]
            dx, dy, dz = xb - xa, yb - ya, zb - za
            r2 = dx * dx + dy * dy + dz * dz
            w = jnp.maximum(1.0 - r2, 0.0)
            if masked:
                least = tile_ref[3 * t + 2] + first
                apart = lax.broadcasted_iota(jnp.int32, (8, 128), 1) - lax.broadcasted_iota(
                    jnp.int32, (8, 128), 0
                )
                w = jnp.where(apart > least, w, 0.0)
            s = lax.rsqrt(r2 + SOFTEN)
            v = s * s
            v3 = v * v * v
            m = c12 * v3
            lj = (m - c6) * v3
            coulomb6 = (qa * qb) * s
            u = 6.0 * coulomb6 + (lj - edge)
            slope = coulomb6 + (lj + m * v3)
            uw = u * w
            energy = energy + uw * w
            g = w * ((1.5 * (w * v)) * slope + u)
            for c, d in enumerate((dx, dy, dz)):
                f = g * d
                other[c] = other[c] + f
                acc_a[p, c, at, :] += f
        for c in range(3):
            acc_b[b, c] += other[c]
        energy_ref[...] += energy

    look_up(0, even_ref)

    @pl.loop(0, cells_a)
    def _(p):
        filled = pack_ref[p, pl.ds(5, 1), pl.ds(0, 1)][0, 0].astype(jnp.int32)
        first, pairs = range_ref[2 * p], range_ref[2 * p + 1]

        def two(i, rows, masked):
            t = 2 * i
            look_up(t + 1, odd_ref)
            tile(p, t, rows, even_ref, masked)
            look_up(t + 2, even_ref)
            tile(p, t + 1, rows, odd_ref, False)

        for rows in range(64, 129, 16):
            fits = filled <= rows
            if rows > 64:
                fits = fits & (filled > rows - 16)

            @pl.when(fits)
            def _(rows=rows):
                two(first, rows, True)

                @pl.loop(1, pairs)
                def _(i):
                    two(first + i, rows, False)

    def sublane_sums(block):
        return jnp.concatenate(
            [jnp.sum(block[c], axis=0, keepdims=True) for c in range(3)]
            + [jnp.zeros((5, 128), jnp.float32)],
            axis=0,
        )

    scale = 4.0 * ENERGY_UNIT

    def finish_a(p):
        turned = [jnp.transpose(acc_a[p, c]) for c in range(3)]
        return (sublane_sums(acc_b[p]) - sublane_sums(turned)) * scale

    @pl.loop(0, shape[1])
    def _(i):
        for j in range(shape[2]):
            force_ref[0, i, j] = finish_a(i * shape[2] + j)

    @pl.loop(0, shape[1])
    def _(i):
        for j in range(shape[2]):
            force_ref[1, i, j] = sublane_sums(acc_b[cells_a + i * shape[2] + j]) * scale


def pair_forces(lists, raw, table):
    tiles, ranges = lists
    shape = raw.shape[:3]
    cells_a = shape[1] * shape[2]
    cells = cells_a * shape[0]
    vmem = pl.BlockSpec(memory_space=pltpu.VMEM)
    smem = pl.BlockSpec(memory_space=pltpu.SMEM)
    return pl.pallas_call(
        functools.partial(pair_kernel, shape),
        out_shape=(
            jax.ShapeDtypeStruct(raw.shape, jnp.float32),
            jax.ShapeDtypeStruct((8, 128), jnp.float32),
        ),
        in_specs=[smem, smem, vmem, vmem],
        out_specs=(vmem, vmem),
        scratch_shapes=[
            pltpu.VMEM((cells + 1, 8, 128), jnp.float32),
            pltpu.VMEM((cells_a, 4, 128, 128), jnp.float32),
            pltpu.VMEM((cells_a, 384, 256), jnp.bfloat16),
            pltpu.VMEM((cells + 1, 256, 128), jnp.bfloat16),
            pltpu.VMEM((cells_a, 3, 128, 128), jnp.float32),
            pltpu.VMEM((cells + 1, 3, 8, 128), jnp.float32),
            pltpu.VMEM((384, 128), jnp.float32),
            pltpu.VMEM((384, 128), jnp.float32),
        ],
        compiler_params=pltpu.CompilerParams(vmem_limit_bytes=56 * 1024 * 1024),
    )(tiles, ranges, raw, table)


AXES = ("gx", "gy", "gz")
CORNERS = ((1, 0, 0), (0, 1, 0), (0, 0, 1), (1, 1, 0), (1, 0, 1), (0, 1, 1), (1, 1, 1))
REACH = 4


def device_at(sizes, offset):
    return {
        axis: lax.rem(lax.axis_index(axis) + offset[k] % sizes[k], sizes[k])
        for k, axis in enumerate(AXES)
        if offset[k] % sizes[k]
    }


def greet(sizes, offsets):
    both = {tuple(o % n for o, n in zip(f, sizes)) for f in offsets}
    both |= {tuple(-o % n for o, n in zip(f, sizes)) for f in offsets}
    both = sorted(both)
    barrier = pltpu.get_barrier_semaphore()
    for offset in both:
        pl.semaphore_signal(
            barrier, inc=1, device_id=device_at(sizes, offset), device_id_type=pl.DeviceIdType.MESH
        )
    pl.semaphore_wait(barrier, len(both))


def send(source, target, send_sem, receive_sem, device):
    copy = pltpu.make_async_remote_copy(
        src_ref=source,
        dst_ref=target,
        send_sem=send_sem,
        recv_sem=receive_sem,
        device_id=device,
        device_id_type=pl.DeviceIdType.MESH,
    )
    copy.start()
    return copy


def import_kernel(sizes, own_ref, whole_ref, local_sem, send_sem, receive_sem):
    ny, nz = own_ref.shape[:2]
    local = pltpu.make_async_copy(own_ref, whole_ref.at[0, pl.ds(0, ny), pl.ds(0, nz)], local_sem)
    local.start()
    greet(sizes, CORNERS)
    copies = []
    for k, (x, y, z) in enumerate(CORNERS):
        ty, tz = (1 if y else ny), (1 if z else nz)
        copies.append(
            send(
                own_ref.at[pl.ds(0, ty), pl.ds(0, tz)],
                whole_ref.at[x, pl.ds(ny if y else 0, ty), pl.ds(nz if z else 0, tz)],
                send_sem.at[k],
                receive_sem.at[k],
                device_at(sizes, (-x, -y, -z)),
            )
        )
    local.wait()
    for copy in copies:
        copy.wait()


def import_cells(own):
    ny, nz = own.shape[:2]
    sizes = tuple(lax.axis_size(a) for a in AXES)
    vmem = pl.BlockSpec(memory_space=pltpu.VMEM)
    return pl.pallas_call(
        functools.partial(import_kernel, sizes),
        out_shape=jax.ShapeDtypeStruct((2, ny + 1, nz + 1) + own.shape[2:], jnp.float32),
        in_specs=[vmem],
        out_specs=vmem,
        scratch_shapes=[
            pltpu.SemaphoreType.DMA,
            pltpu.SemaphoreType.DMA((len(CORNERS),)),
            pltpu.SemaphoreType.DMA((len(CORNERS),)),
        ],
        compiler_params=pltpu.CompilerParams(collective_id=0, has_side_effects=True),
    )(own)


def export_kernel(
    sizes, force_ref, energy_ref, total_ref, sum_ref,
    r0, r1, r2, r3, r4, r5, r6, line_ref, column_ref, plane_ref,
    send_sem, receive_sem, line_send, line_receive, plane_send, plane_receive,
):
    nx, gy, gz = sizes
    ny, nz = total_ref.shape[:2]
    arrivals = (r0, r1, r2, r3, r4, r5, r6)
    plane = [(0, y, z) for y in range(gy) for z in range(gz) if (y, z) != (0, 0)]
    centre = nx // 2 - 1
    greet(sizes, list(CORNERS) + [(d, 0, 0) for d in range(1, REACH + 1)] + plane)
    lines = []

    def line(source, target, offset):
        k = len(lines)
        lines.append(
            send(source, target, line_send.at[k], line_receive.at[k], device_at(sizes, (offset, 0, 0)))
        )

    for d in range(1, REACH + 1):
        line(energy_ref, line_ref.at[centre + d], -d)
        line(energy_ref, line_ref.at[centre - d], d)
    copies = []
    for k, (x, y, z) in enumerate(CORNERS):
        copies.append(
            send(
                force_ref.at[
                    x, pl.ds(ny if y else 0, 1 if y else ny), pl.ds(nz if z else 0, 1 if z else nz)
                ],
                arrivals[k],
                send_sem.at[k],
                receive_sem.at[k],
                device_at(sizes, (x, y, z)),
            )
        )
    line_ref[centre] = energy_ref[...]
    begun = 0
    for stage in range(1, nx // 2 // REACH):
        waited = len(lines)
        for copy in lines[begun:waited]:
            copy.wait()
        begun = waited
        first = REACH * (stage - 1)
        line(
            line_ref.at[pl.ds(centre + first + 1, REACH)],
            line_ref.at[pl.ds(centre + first + 1 + REACH, REACH)],
            -REACH,
        )
        count = REACH - (1 if stage == nx // 2 // REACH - 1 else 0)
        line(
            line_ref.at[pl.ds(centre - first - count, count)],
            line_ref.at[pl.ds(centre - first - count - REACH, count)],
            REACH,
        )
        if stage == 1:
            for copy in copies:
                copy.wait()
            for y in range(ny):
                for z in range(nz):
                    total = force_ref[0, y, z]
                    for k, (_, cy, cz) in enumerate(CORNERS):
                        if (y == 0 or not cy) and (z == 0 or not cz):
                            total = total + arrivals[k][y, z]
                    total_ref[y, z] = total[:3]
    for copy in lines[begun:]:
        copy.wait()
    me = lax.axis_index("gx")
    column = jnp.zeros((8, 128), jnp.float32)
    for i in range(nx):
        column = column + line_ref[lax.rem(centre + i + nx - me, nx)]
    column_ref[...] = column
    mine = lax.axis_index("gy") * gz + lax.axis_index("gz")
    planes = [
        send(column_ref, plane_ref.at[mine], plane_send.at[k], plane_receive.at[k], device_at(sizes, o))
        for k, o in enumerate(plane)
    ]
    plane_ref[mine] = column
    for copy in planes:
        copy.wait()
    total = plane_ref[0]
    for k in range(1, gy * gz):
        total = total + plane_ref[k]
    sum_ref[...] = jnp.broadcast_to(ENERGY_UNIT * jnp.sum(total, keepdims=True), (8, 128))


def export(forces, energy, slots):
    ny, nz = forces.shape[1] - 1, forces.shape[2] - 1
    sizes = tuple(lax.axis_size(a) for a in AXES)
    vmem = pl.BlockSpec(memory_space=pltpu.VMEM)
    lines = 2 * REACH + 2 * (sizes[0] // 2 // REACH - 1)
    dma = pltpu.SemaphoreType.DMA
    return pl.pallas_call(
        functools.partial(export_kernel, sizes),
        out_shape=(
            jax.ShapeDtypeStruct((ny, nz, 3, slots), jnp.float32),
            jax.ShapeDtypeStruct((8, 128), jnp.float32),
        ),
        in_specs=[vmem, vmem],
        out_specs=(vmem, vmem),
        scratch_shapes=[
            pltpu.VMEM((1 if y else ny, 1 if z else nz, 8, slots), jnp.float32) for _, y, z in CORNERS
        ]
        + [
            pltpu.VMEM((sizes[0], 8, 128), jnp.float32),
            pltpu.VMEM((8, 128), jnp.float32),
            pltpu.VMEM((sizes[1] * sizes[2], 8, 128), jnp.float32),
            dma((len(CORNERS),)),
            dma((len(CORNERS),)),
            dma((lines,)),
            dma((lines,)),
            dma((sizes[1] * sizes[2],)),
            dma((sizes[1] * sizes[2],)),
        ],
        compiler_params=pltpu.CompilerParams(collective_id=1, has_side_effects=True),
    )(forces, energy)


def on_device(coords, charges, atom_types, counts, c6_table, c12_table):
    ny, nz, slots = coords.shape[1], coords.shape[2], coords.shape[4]
    filled = jnp.arange(slots, dtype=jnp.int32) < counts[..., None]
    own = jnp.concatenate(
        [
            coords,
            jnp.where(filled, charges, 0.0)[..., None, :],
            jnp.where(filled, atom_types, 64).astype(jnp.float32)[..., None, :],
            jnp.broadcast_to(counts.astype(jnp.float32)[..., None, None], counts.shape + (1, slots)),
            jnp.zeros(counts.shape + (2, slots), jnp.float32),
        ],
        axis=3,
    )[0]
    raw = import_cells(own)
    types = c6_table.shape[0]
    both = jnp.stack([0.5 * (c6_table + c6_table.T), 0.5 * (c12_table + c12_table.T)], axis=1)
    both = jnp.concatenate([both, both], axis=2)
    both = jnp.pad(both, ((0, 128 - types), (0, 0), (0, 0))).reshape(128, 256)
    high = lax.reduce_precision(both, 8, 7)
    table = jnp.concatenate([high, both - high]).astype(jnp.bfloat16)
    lists = tuple(jnp.asarray(k) for k in neighbour_lists(ny, nz))
    forces, energy = pair_forces(lists, raw, table)
    total, energy_sum = export(forces, energy, slots)
    return (total[None], energy_sum[0, :1])


def solution(mesh):
    return jax.shard_map(
        on_device,
        mesh=mesh,
        in_specs=(
            P(("groups", "gx"), "gy", "gz", None, None),
            P(("groups", "gx"), "gy", "gz", None),
            P(("groups", "gx"), "gy", "gz", None),
            P(("groups", "gx"), "gy", "gz"),
            P(),
            P(),
        ),
        out_specs=(P(("groups", "gx"), "gy", "gz", None, None), P("groups")),
        check_vma=False,
    )
```

time: 450 us -> 182 us (0.40); the launches traced: 442 us -> 182 us
  Pallas kernels: 0 us -> 173 us
  matrix products: 167 us -> 0 us
  other arithmetic: 96.1 us -> 1.61 us
  blocking collectives: 71.1 us -> 0 us
  starting transfers between devices: 61.3 us -> 0 us
  local copies, waits for them, and re-layouts: 20.9 us -> 5.77 us
  between operations: 11.4 us -> 0.74 us
  loops' own time: 8.36 us -> 0 us
  waiting for transfers between devices: 6.18 us -> 0 us
    pallas_call x0 -> x3, Pallas kernels: none -> 173 us  [the longest x1 87.7 us: pair_forces(): pl.pallas_call(functools.partial(pair_kernel, shape), out_shape=(jax.Shap...]
    dot_general x224 -> x0, matrix products: 167 us -> none  [the longest x56 92.9 us: tile_terms(): jnp.dot(jnp.dot(type_hot_a, c12_sym, precision=lax.Precision.HIGHEST), ty...]
    reduce_sum x126 -> x0, other arithmetic: 91 us -> none  [the longest x56 55.2 us: pair_energy(): position_b[:, None, :] - position_a[:, :, None] + offset[:, None, None]]
    psum x3 -> x0, blocking collectives: 71.1 us -> none  [over_axes(): shard = lax.psum(shard, axis)]
    ppermute x6 -> x0, starting transfers between devices: 61.3 us -> none  [shifted(): return lax.ppermute(block, axis, route)]
    another operation x14 -> x0, loops' own time: 8.36 us -> none  [cell_batch(): return lax.map(single, (packs_a, packs_b), batch_size=8)]
    dynamic_update_slice x164 -> x0, local copies, waits for them, and re-layouts: 7.51 us -> none  [cell_batch(): return lax.map(single, (packs_a, packs_b), batch_size=8)]
    ppermute x6 -> x0, waiting for transfers between devices: 6.18 us -> none  [shifted(): return lax.ppermute(block, axis, route)]
  transfers between devices with their start and end apart: 6 -> 0, of which waited for: 3 -> 0; matrix products, arithmetic and copies ran while one was open for 7% -> 0% of each run, Pallas kernels for 0% -> 0%
where the time goes in v1:
time: 182 us
  Pallas kernels  173 us (95%)
  local copies, waits for them, and re-layouts  5.77 us (3%)
    pallas_call x1, Pallas kernels, pair_forces(): pl.pallas_call(functools.partial(pair_kernel, shape), out_shape=(jax.Shap...  87.7 us
    pallas_call x1, Pallas kernels, import_cells(): pl.pallas_call(functools.partial(import_kernel, sizes), out_shape=jax.Sha...  53.6 us
    pallas_call x1, Pallas kernels, export(): pl.pallas_call(functools.partial(export_kernel, sizes), out_shape=(jax.Sh...  32.2 us
    unnamed x17, local copies, waits for them, and re-layouts  3.69 us

profile of v1, /device:TPU:33, one launch (start us, length us, event | category | flops | bytes accessed | tf_op | source)
XLA Modules:
  0.0 181.6 jit_solution(1169810010451221543)
XLA Ops:
  0.6 0.0 copy-start.4
  0.6 0.7 convert_bitcast_fusion
  1.3 0.0 copy-start.5
  1.3 0.1 broadcast_in_dim.35
  1.4 0.0 copy-done.4
  1.4 0.6 copy-done.3
  2.0 0.1 fusion.5
  2.1 0.0 copy-done.5
  2.1 0.1 select_convert_fusion
  2.2 0.6 copy-done.1
  2.8 0.1 copy.12
  2.8 0.7 copy-done
  3.5 0.1 copy.13
  3.6 0.1 maximum_maximum_fusion
  3.7 0.1 copy.16
  3.9 0.0 copy-start.2
  3.9 0.7 pad_maximum_fusion.table_ref
  4.5 0.1 copy-done.2
  4.7 0.8 concatenate.10
  5.5 53.6 %shard_map.95.raw_ref = f32[2,5,9,8,128]{4,3,2,1,0:T(8,128)} custom-call(f32[4,8,8,128]{3,2,1,0:T(8,128)} %bitcast.31), custom_call_target="tpu_custom_call" | custom-call | tf_op jit(solution)/shard_map/pallas_call | solution.py:319
  59.1 87.7 %shard_map.96 = (f32[2,5,9,8,128]{4,3,2,1,0:T(8,128)}, f32[8,128]{1,0:T(8,128)}) custom-call(s32[1395]{0:T(1024)} %constant.4.clone.tile_ref, s32[90]{0:T(128)} %constant.14.clone.range_ref, f32[2,5,9,8,128]{4,3,2,1,0:T(8,128)} %shard_map.95.raw_ref, bf16[256,256]{1,0:T(8,128)(2,1)} %pad_maximum_fusion.table_ref), custom_call_target="tpu_custom_call" | custom-call | tf_op jit(solution)/shard_map/pallas_call | solution.py:233
  146.8 32.2 %shard_map.97 = (f32[4,8,3,128]{3,2,1,0:T(4,128)}, f32[8,128]{1,0:T(8,128)}) custom-call(f32[2,5,9,8,128]{4,3,2,1,0:T(8,128)} %get-tuple-element.6.force_ref, f32[8,128]{1,0:T(8,128)} %get-tuple-element.7.energy_ref), custom_call_target="tpu_custom_call" | custom-call | tf_op jit(solution)/shard_map/pallas_call | solution.py:424
  179.0 1.2 slice.3
  180.2 1.5 copy.15
  (8 shorter events, 0.1 us)
Async XLA Ops:
  0.6 0.8 copy-start.4
  1.3 0.7 copy-start.3
  1.3 0.8 copy-start.5
  2.0 0.8 copy-start.1
  2.8 0.8 copy-start
  3.9 0.8 copy-start.2

commit v2 on v1

--- a/solution.py
+++ b/solution.py
@@ -46,7 +46,7 @@
                 partners.append((empty, -1024))
             ranges.append((len(tiles) // 2, len(partners) // 2))
             tiles += [(p, b, below) for b, below in partners]
-    tiles.append((0, empty, 0))
+    tiles += [(0, empty, 0)] * 2
     return np.array(tiles, np.int32).reshape(-1), np.array(ranges, np.int32).reshape(-1)
 
 
@@ -57,7 +57,7 @@
 
 def pair_kernel(
     shape, tile_ref, range_ref, raw_ref, table_ref, force_ref, energy_ref,
-    pack_ref, col_ref, left_ref, right_ref, acc_a, acc_b, even_ref, odd_ref,
+    pack_ref, col_ref, left_ref, right_ref, acc_a, acc_b, *found,
 ):
     iota = functools.partial(lax.broadcasted_iota, jnp.int32, (128, 128))
     row = lax.broadcasted_iota(jnp.int32, (8, 128), 0)
@@ -70,48 +70,33 @@
                 pack_ref[(x * shape[1] + y) * shape[2] + z] = raw_ref[x, y, z] + CELL_EDGE * place
     pack_ref[cells] = jnp.where(row == 4, 64.0, 0.0)
 
+    def column(p, f):
+        return jnp.transpose(jnp.broadcast_to(pack_ref[p, pl.ds(f, 1), :], (128, 128)))
+
     def prepare_a(p):
-        turned = jnp.transpose(pack_ref[p])
-        for f in range(3):
-            col_ref[p, f] = jnp.broadcast_to(turned[:, f : f + 1], (128, 128))
-        qa = jnp.broadcast_to(turned[:, 3:4], (128, 128))
-        col_ref[p, 3] = qa * (1.0 / 6.0)
-        kinds = jnp.broadcast_to(turned[:, 4:5], (128, 128))
-        hot = jnp.where(kinds == iota(1).astype(jnp.float32), 1.0, 0.0).astype(jnp.bfloat16)
+        for f in range(4):
+            col_ref[p, f] = column(p, f)
+        hot = jnp.where(column(p, 4) == iota(1).astype(jnp.float32), 1.0, 0.0).astype(jnp.bfloat16)
         rows = jnp.dot(
             jnp.concatenate([hot, hot], axis=1), table_ref[...], preferred_element_type=jnp.float32
         )
         r6, r12 = rows[:, :128], rows[:, 128:]
         low_half = iota(1) < 64
-        empty = jnp.zeros((128, 128), jnp.bfloat16)
 
         def halves(value):
             high = value.astype(jnp.bfloat16).astype(jnp.float32)
             return jnp.where(low_half, high, value - high).astype(jnp.bfloat16)
 
-        left_ref[p, :128, :128] = halves(r6)
-        left_ref[p, :128, 128:] = empty
-        left_ref[p, 128:256, :128] = halves(r12)
-        left_ref[p, 128:256, 128:] = empty
-        left_ref[p, 256:, :128] = halves(EDGE_CUBE * EDGE_CUBE * r12 - EDGE_CUBE * r6)
-        qs = qa * EDGE_ROOT
-        high = qs.astype(jnp.bfloat16).astype(jnp.float32)
-        lane = iota(1)
-        left_ref[p, 256:, 128:] = jnp.where(
-            lane < 4, jnp.where((lane & 1) == 0, high, qs - high), 0.0
-        ).astype(jnp.bfloat16)
+        for k, value in enumerate((r6, r12, EDGE_CUBE * EDGE_CUBE * r12 - EDGE_CUBE * r6)):
+            both = halves(value)
+            for first in range(0, 128, 16):
+                at = 3 * first + 16 * k
+                left_ref[p, at : at + 16] = both[first : first + 16]
         acc_a[p] = jnp.zeros((3, 128, 128), jnp.float32)
 
     def prepare_b(b):
         kinds = jnp.broadcast_to(pack_ref[b, pl.ds(4, 1), :].astype(jnp.int32), (128, 128))
-        hot = jnp.where((iota(0) & 63) == kinds, 1.0, 0.0)
-        right_ref[b, :128] = hot.astype(jnp.bfloat16)
-        q = jnp.broadcast_to(pack_ref[b, pl.ds(3, 1), :], (16, 128))
-        high = q.astype(jnp.bfloat16).astype(jnp.float32)
-        row = lax.broadcasted_iota(jnp.int32, (16, 128), 0)
-        q = jnp.where(row < 2, high, jnp.where(row < 4, q - high, 0.0))
-        right_ref[b, 128:144] = q.astype(jnp.bfloat16)
-        right_ref[b, 144:] = jnp.zeros((112, 128), jnp.bfloat16)
+        right_ref[b] = jnp.where((iota(0) & 63) == kinds, 1.0, 0.0).astype(jnp.bfloat16)
         acc_b[b] = jnp.zeros((3, 8, 128), jnp.float32)
 
     step = 3
@@ -129,9 +114,11 @@
     prepare_b(cells)
     energy_ref[...] = jnp.zeros((8, 128), jnp.float32)
 
-    def look_up(t, out_ref):
+    def look_up(t, out_ref, rows):
         p, b = tile_ref[3 * t], tile_ref[3 * t + 1]
-        out_ref[...] = jnp.dot(left_ref[p], right_ref[b], preferred_element_type=jnp.float32)
+        out_ref[: 3 * rows] = jnp.dot(
+            left_ref[p, : 3 * rows], right_ref[b], preferred_element_type=jnp.float32
+        )
 
     def tile(p, t, rows, in_ref, masked):
         b = tile_ref[3 * t + 1]
@@ -141,9 +128,8 @@
         for first in range(0, rows, 8):
             at = slice(first, first + 8)
             xa, ya, za, qa = (col_ref[p, f, at, :] for f in range(4))
-            c6 = in_ref[first : first + 8, :]
-            c12 = in_ref[128 + first : 136 + first, :]
-            edge = in_ref[256 + first : 264 + first, :]
+            found_at = 3 * (first - first % 16) + first % 16
+            c6, c12, edge = (in_ref[found_at + 16 * k : found_at + 16 * k + 8, :] for k in range(3))
             dx, dy, dz = xb - xa, yb - ya, zb - za
             r2 = dx * dx + dy * dy + dz * dz
             w = jnp.maximum(1.0 - r2, 0.0)
@@ -158,9 +144,10 @@
             v3 = v * v * v
             m = c12 * v3
             lj = (m - c6) * v3
-            coulomb6 = (qa * qb) * s
-            u = 6.0 * coulomb6 + (lj - edge)
-            slope = coulomb6 + (lj + m * v3)
+            charge = qa * qb
+            coulomb = charge * s
+            u = (coulomb - charge * EDGE_ROOT) + (lj - edge)
+            slope = coulomb * (1.0 / 6.0) + (lj + m * v3)
             uw = u * w
             energy = energy + uw * w
             g = w * ((1.5 * (w * v)) * slope + u)
@@ -172,32 +159,35 @@
             acc_b[b, c] += other[c]
         energy_ref[...] += energy
 
-    look_up(0, even_ref)
+    for k in range(2):
+        look_up(k, found[k], 128)
 
     @pl.loop(0, cells_a)
     def _(p):
         filled = pack_ref[p, pl.ds(5, 1), pl.ds(0, 1)][0, 0].astype(jnp.int32)
         first, pairs = range_ref[2 * p], range_ref[2 * p + 1]
 
-        def two(i, rows, masked):
-            t = 2 * i
-            look_up(t + 1, odd_ref)
-            tile(p, t, rows, even_ref, masked)
-            look_up(t + 2, even_ref)
-            tile(p, t + 1, rows, odd_ref, False)
-
-        for rows in range(64, 129, 16):
-            fits = filled <= rows
-            if rows > 64:
-                fits = fits & (filled > rows - 16)
+        def two(i, rows, next_rows):
+            for turn in range(2):
+
+                @pl.when((i & 1) == turn)
+                def _(turn=turn):
+                    for k in range(2):
+                        look_up(2 * i + 2 + k, found[2 - 2 * turn + k], next_rows)
+                    for k in range(2):
+                        tile(p, 2 * i + k, rows, found[2 * turn + k], k == 0)
+
+        steps = (96, 128)
+        for least, rows in zip((0,) + steps, steps):
+            fits = (filled <= rows) & (filled > least)
 
             @pl.when(fits)
             def _(rows=rows):
-                two(first, rows, True)
-
-                @pl.loop(1, pairs)
+                @pl.loop(0, pairs - 1)
                 def _(i):
-                    two(first + i, rows, False)
+                    two(first + i, rows, rows)
+
+                two(first + pairs - 1, rows, 128)
 
     def sublane_sums(block):
         return jnp.concatenate(
@@ -241,13 +231,12 @@
         scratch_shapes=[
             pltpu.VMEM((cells + 1, 8, 128), jnp.float32),
             pltpu.VMEM((cells_a, 4, 128, 128), jnp.float32),
-            pltpu.VMEM((cells_a, 384, 256), jnp.bfloat16),
-            pltpu.VMEM((cells + 1, 256, 128), jnp.bfloat16),
+            pltpu.VMEM((cells_a, 384, 128), jnp.bfloat16),
+            pltpu.VMEM((cells + 1, 128, 128), jnp.bfloat16),
             pltpu.VMEM((cells_a, 3, 128, 128), jnp.float32),
             pltpu.VMEM((cells + 1, 3, 8, 128), jnp.float32),
-            pltpu.VMEM((384, 128), jnp.float32),
-            pltpu.VMEM((384, 128), jnp.float32),
-        ],
+        ]
+        + [pltpu.VMEM((384, 128), jnp.float32)] * 4,
         compiler_params=pltpu.CompilerParams(vmem_limit_bytes=56 * 1024 * 1024),
     )(tiles, ranges, raw, table)
 
@@ -290,10 +279,8 @@
     return copy
 
 
-def import_kernel(sizes, own_ref, whole_ref, local_sem, send_sem, receive_sem):
+def import_kernel(sizes, own_ref, whole_ref, send_sem, receive_sem):
     ny, nz = own_ref.shape[:2]
-    local = pltpu.make_async_copy(own_ref, whole_ref.at[0, pl.ds(0, ny), pl.ds(0, nz)], local_sem)
-    local.start()
     greet(sizes, CORNERS)
     copies = []
     for k, (x, y, z) in enumerate(CORNERS):
@@ -307,7 +294,7 @@
                 device_at(sizes, (-x, -y, -z)),
             )
         )
-    local.wait()
+    whole_ref[0, :ny, :nz] = own_ref[...]
     for copy in copies:
         copy.wait()
 
@@ -322,7 +309,6 @@
         in_specs=[vmem],
         out_specs=vmem,
         scratch_shapes=[
-            pltpu.SemaphoreType.DMA,
             pltpu.SemaphoreType.DMA((len(CORNERS),)),
             pltpu.SemaphoreType.DMA((len(CORNERS),)),
         ],

time: 182 us -> 160 us (0.88)
  Pallas kernels: 173 us -> 151 us
    pallas_call x1, Pallas kernels: 87.7 us -> 66.5 us  [pair_forces(): pl.pallas_call(functools.partial(pair_kernel, shape), out_shape=(jax.Shap...]
where the time goes in v2:
time: 160 us; the launch traced here: 159 us
  Pallas kernels  151 us (94%)
  local copies, waits for them, and re-layouts  5.77 us (4%)
  other arithmetic  1.61 us (1%)
    pallas_call x1, Pallas kernels, pair_forces(): pl.pallas_call(functools.partial(pair_kernel, shape), out_shape=(jax.Shap...  66.5 us
    pallas_call x1, Pallas kernels, import_cells(): pl.pallas_call(functools.partial(import_kernel, sizes), out_shape=jax.Sha...  53.4 us
    pallas_call x1, Pallas kernels, export(): pl.pallas_call(functools.partial(export_kernel, sizes), out_shape=(jax.Sh...  31.4 us
    unnamed x17, local copies, waits for them, and re-layouts  3.69 us

profile of v2, /device:TPU:33, one launch (start us, length us, event | category | flops | bytes accessed | tf_op | source)
XLA Modules:
  0.0 159.4 jit_solution(13903729384925587651)
XLA Ops:
  0.6 0.0 copy-start.4
  0.6 0.7 convert_bitcast_fusion
  1.3 0.0 copy-start.3
  1.3 0.1 broadcast_in_dim.35
  1.4 0.0 copy-done.4
  1.4 0.6 copy-done.3
  2.0 0.1 fusion.5
  2.1 0.0 copy-done.5
  2.1 0.1 select_convert_fusion
  2.2 0.6 copy-done.1
  2.8 0.1 copy.12
  2.8 0.7 copy-done
  3.5 0.1 copy.13
  3.6 0.1 maximum_maximum_fusion
  3.7 0.1 copy.16
  3.9 0.0 copy-start.2
  3.9 0.7 pad_maximum_fusion.table_ref
  4.5 0.1 copy-done.2
  4.7 0.8 concatenate.10
  5.5 53.4 %shard_map.95.raw_ref = f32[2,5,9,8,128]{4,3,2,1,0:T(8,128)} custom-call(f32[4,8,8,128]{3,2,1,0:T(8,128)} %bitcast.31), custom_call_target="tpu_custom_call" | custom-call | tf_op jit(solution)/shard_map/pallas_call | solution.py:306
  58.8 66.5 %shard_map.96 = (f32[2,5,9,8,128]{4,3,2,1,0:T(8,128)}, f32[8,128]{1,0:T(8,128)}) custom-call(s32[1398]{0:T(1024)} %constant.4.clone.tile_ref, s32[90]{0:T(128)} %constant.14.clone.range_ref, f32[2,5,9,8,128]{4,3,2,1,0:T(8,128)} %shard_map.95.raw_ref, bf16[256,256]{1,0:T(8,128)(2,1)} %pad_maximum_fusion.table_ref), custom_call_target="tpu_custom_call" | custom-call | tf_op jit(solution)/shard_map/pallas_call | solution.py:223
  125.4 31.4 %shard_map.97 = (f32[4,8,3,128]{3,2,1,0:T(4,128)}, f32[8,128]{1,0:T(8,128)}) custom-call(f32[2,5,9,8,128]{4,3,2,1,0:T(8,128)} %get-tuple-element.6.force_ref, f32[8,128]{1,0:T(8,128)} %get-tuple-element.7.energy_ref), custom_call_target="tpu_custom_call" | custom-call | tf_op jit(solution)/shard_map/pallas_call | solution.py:410
  156.8 1.2 slice.3
  157.9 1.5 copy.15
  (8 shorter events, 0.1 us)
Async XLA Ops:
  0.6 0.8 copy-start.4
  1.3 0.7 copy-start.3
  1.3 0.8 copy-start.5
  2.0 0.8 copy-start.1
  2.8 0.8 copy-start
  3.9 0.8 copy-start.2

commit v3 on v2

--- a/solution.py
+++ b/solution.py
@@ -243,7 +243,7 @@
 
 AXES = ("gx", "gy", "gz")
 CORNERS = ((1, 0, 0), (0, 1, 0), (0, 0, 1), (1, 1, 0), (1, 0, 1), (0, 1, 1), (1, 1, 1))
-REACH = 4
+REACH = 8
 
 
 def device_at(sizes, offset):

time: 160 us -> 158 us (0.988)
  no operation moved by 1% of the time
where the time goes in v3:
time: 158 us
  Pallas kernels  150 us (95%)
  local copies, waits for them, and re-layouts  5.77 us (4%)
  other arithmetic  1.61 us (1%)
    pallas_call x1, Pallas kernels, pair_forces(): pl.pallas_call(functools.partial(pair_kernel, shape), out_shape=(jax.Shap...  66.7 us
    pallas_call x1, Pallas kernels, import_cells(): pl.pallas_call(functools.partial(import_kernel, sizes), out_shape=jax.Sha...  53.4 us
    pallas_call x1, Pallas kernels, export(): pl.pallas_call(functools.partial(export_kernel, sizes), out_shape=(jax.Sh...  30.2 us
    unnamed x17, local copies, waits for them, and re-layouts  3.69 us

profile of v3, /device:TPU:33, one launch (start us, length us, event | category | flops | bytes accessed | tf_op | source)
XLA Modules:
  0.0 158.4 jit_solution(12059048904172109362)
XLA Ops:
  0.6 0.0 copy-start.4
  0.6 0.7 convert_bitcast_fusion
  1.3 0.0 copy-start.3
  1.3 0.1 broadcast_in_dim.35
  1.4 0.0 copy-done.4
  1.4 0.6 copy-done.3
  2.0 0.1 fusion.5
  2.1 0.0 copy-done.5
  2.1 0.1 select_convert_fusion
  2.2 0.6 copy-done.1
  2.8 0.1 copy.12
  2.8 0.7 copy-done
  3.5 0.1 copy.13
  3.6 0.1 maximum_maximum_fusion
  3.7 0.1 copy.16
  3.9 0.0 copy-start.2
  3.9 0.7 pad_maximum_fusion.table_ref
  4.5 0.1 copy-done.2
  4.7 0.8 concatenate.10
  5.5 53.4 %shard_map.95.raw_ref = f32[2,5,9,8,128]{4,3,2,1,0:T(8,128)} custom-call(f32[4,8,8,128]{3,2,1,0:T(8,128)} %bitcast.31), custom_call_target="tpu_custom_call" | custom-call | tf_op jit(solution)/shard_map/pallas_call | solution.py:306
  58.8 66.7 %shard_map.96 = (f32[2,5,9,8,128]{4,3,2,1,0:T(8,128)}, f32[8,128]{1,0:T(8,128)}) custom-call(s32[1398]{0:T(1024)} %constant.4.clone.tile_ref, s32[90]{0:T(128)} %constant.14.clone.range_ref, f32[2,5,9,8,128]{4,3,2,1,0:T(8,128)} %shard_map.95.raw_ref, bf16[256,256]{1,0:T(8,128)(2,1)} %pad_maximum_fusion.table_ref), custom_call_target="tpu_custom_call" | custom-call | tf_op jit(solution)/shard_map/pallas_call | solution.py:223
  125.6 30.2 %shard_map.97 = (f32[4,8,3,128]{3,2,1,0:T(4,128)}, f32[8,128]{1,0:T(8,128)}) custom-call(f32[2,5,9,8,128]{4,3,2,1,0:T(8,128)} %get-tuple-element.6.force_ref, f32[8,128]{1,0:T(8,128)} %get-tuple-element.7.energy_ref), custom_call_target="tpu_custom_call" | custom-call | tf_op jit(solution)/shard_map/pallas_call | solution.py:410
  155.8 1.2 slice.3
  156.9 1.5 copy.15
  (8 shorter events, 0.1 us)
Async XLA Ops:
  0.6 0.8 copy-start.4
  1.3 0.7 copy-start.3
  1.3 0.8 copy-start.5
  2.0 0.8 copy-start.1
  2.8 0.8 copy-start
  3.9 0.8 copy-start.2
